TPU v7x, 32 devices: a whole 2x2x4 slice. The times are simulated.
32 devices in a mesh: groups: 2 (over y), seq: 4 (over z), tp: 2 (over x), ref: 2 (over core).
Axes of the slice: x: 2, y: 2, z: 4, core: 2. Of those that a mesh axis runs over, the one named last changes fastest.
Arguments:
- hidden: bfloat16 [2, 2048, 4096], P('ref', ('groups', 'seq'), 'tp'), parts along dimension 1, may hold values from -6 to 6
- segment_ids: int32 [2048], P(('groups', 'seq')), parts along dimension 0, may hold values from 0 to 3, never falling along the last dimension, each value on 1 to 768 neighbouring positions
- targets: int32 [2048], P(('groups', 'seq')), parts along dimension 0, may hold values from 0 to 4095
- loss_mask: int32 [2048], P(('groups', 'seq')), parts along dimension 0, may hold values from 0 to 1, as said below
- attn_gain: float32 [2, 4096], P('ref'), may hold values from 0.5 to 2
- final_gain: float32 [2, 4096], P('ref'), may hold values from 1 to 4
- w_query: bfloat16 [2, 4096, 2048], P('ref', 'seq', 'tp'), may hold values from -0.125 to 0.125
- w_key: bfloat16 [2, 4096, 1024], P('ref', 'seq', 'tp'), may hold values from -0.125 to 0.125
- w_value: bfloat16 [2, 4096, 1024], P('ref', 'seq', 'tp'), may hold values from -0.09375 to 0.09375
- w_out: bfloat16 [2, 2048, 4096], P('ref', 'tp', 'seq'), may hold values from -0.125 to 0.125
- head: bfloat16 [2, 4096, 4096], P('ref', None, ('seq', 'tp')), may hold values from -0.25784398 to 0.25784398
Outputs:
- logprobs: float32 [2, 2048], P('ref', ('groups', 'seq')), parts along dimension 1
There are 2 independent parts, one for each index of `groups`. A program takes and returns all parts, laid end to end along the dimension named above; an argument that names none is the same for every part. Nothing has to cross between parts.
Inputs may be any that keep to these rules, and one draw needn't show every extreme that they name: `loss_mask`: each aligned block of 256 positions holds 1 to 32 positions with mask 1, and some block holds exactly 32. `segment_ids`: never falling; every rollout number appears; the longest rollout holds exactly 768 positions.
All inputs are finite; a program needn't handle non-finite values.
Results may differ from a plain program's by a relative error of at most 0.0003.
Values may be sent and summed in bfloat16 or wider, within the bound.
A program may use at most 128 MiB of HBM per device.

v0:
```python
import functools

import jax
import jax.numpy as jnp
from jax import lax
from jax.experimental import pallas as pl
from jax.experimental.pallas import tpu as pltpu
from jax.sharding import PartitionSpec as P

HEAD_DIM = 128
WINDOW = 2048
CAP = 32
SEGMENTS = 4


EPS = 1e-05
THETA = 500000.0
FARTHEST = 1073741824


def passed_along(value, axis, by):
    length = lax.axis_size(axis)
    pairs = [(i, i + by) for i in range(length) if 0 <= i + by < length]
    return lax.ppermute(value, axis, pairs)


def joined(part, axis, combine):
    gathered = jax.tree.map(lambda a: lax.all_gather(a, axis), part)

    def take(source):
        return jax.tree.map(lambda a: lax.dynamic_index_in_dim(a, source, 0, False), gathered)

    return lax.fori_loop(
        1, lax.axis_size(axis), lambda source, state: combine(state, take(source)), take(0)
    )


def rms_norm(values, gain):
    return values * lax.rsqrt(jnp.mean(values * values, axis=-1, keepdims=True) + EPS) * gain


def rotate(tensor, offsets):
    half = tensor.shape[-1] // 2
    freq = THETA ** (-(jnp.arange(half, dtype=jnp.float32) * 2.0 / tensor.shape[-1]))
    angle = offsets.astype(jnp.float32)[:, None] * freq[None, :]
    cosine = jnp.cos(angle)[:, None, :]
    sine = jnp.sin(angle)[:, None, :]
    first = tensor[..., :half]
    second = tensor[..., half:]
    return jnp.concatenate(
        [first * cosine - second * sine, second * cosine + first * sine], axis=-1
    )


def combine_stats(left, right):
    top = jnp.maximum(left[0], right[0])
    total = left[1] * jnp.exp(left[0] - top) + right[1] * jnp.exp(right[0] - top)
    return (top, total, left[2] + right[2])


def block_stats(scores, allowed):
    row_peak = jnp.max(scores, axis=-1)
    lifted = jnp.where(allowed[None, None, :, :], jnp.exp(scores - row_peak[..., None]), 0.0)
    return (row_peak, jnp.sum(lifted, axis=-1))


def weighted_values(scores, row_peak, row_total, value_block):
    safe_total = jnp.where(row_total > 0.0, row_total, 1.0)
    weights = (jnp.exp(scores - row_peak[..., None]) / safe_total[..., None]).astype(jnp.bfloat16)
    return jnp.einsum("ngck,knd->cngd", weights, value_block, preferred_element_type=jnp.float32)


def gathered_weights(
    hidden,
    segment_ids,
    targets,
    loss_mask,
    attn_gain,
    final_gain,
    w_query,
    w_key,
    w_value,
    w_out,
    head,
):
    tokens = hidden.shape[1]
    seq_index = lax.axis_index("seq")
    base = seq_index * tokens
    position = base + jnp.arange(tokens, dtype=jnp.int32)
    whole = lax.all_gather(hidden[0], "tp", axis=1, tiled=True)
    xfloat = whole.astype(jnp.float32)
    normed = rms_norm(xfloat, attn_gain[0]).astype(jnp.bfloat16)
    labels = jnp.arange(SEGMENTS, dtype=jnp.int32)
    member = segment_ids[None, :] == labels[:, None]
    local_first = jnp.min(jnp.where(member, position[None, :], FARTHEST), axis=1)
    starts = lax.pmin(local_first, "seq")
    token_start = jnp.sum(jnp.where(member, starts[:, None], 0), axis=0)
    offsets = position - token_start
    ranking = jnp.cumsum(loss_mask) - 1
    picks = (loss_mask[None, :] == 1) & (
        ranking[None, :] == jnp.arange(CAP, dtype=jnp.int32)[:, None]
    )
    chooser = picks.astype(jnp.bfloat16)
    normed_rows = jnp.dot(chooser, normed, preferred_element_type=jnp.float32).astype(jnp.bfloat16)
    x_rows = jnp.dot(chooser, whole, preferred_element_type=jnp.float32)
    row_pos = jnp.sum(jnp.where(picks, position[None, :], 0), axis=1)
    row_start = jnp.sum(jnp.where(picks, token_start[None, :], 0), axis=1)
    row_target = jnp.sum(jnp.where(picks, targets[None, :], 0), axis=1)
    places = jnp.stack([row_pos, row_start])
    query_cols = w_query.shape[2]
    key_cols = w_key.shape[2]
    local_heads = query_cols // HEAD_DIM
    local_kv = key_cols // HEAD_DIM
    group = local_heads // local_kv
    score_scale = HEAD_DIM ** (-0.5)
    query = jnp.dot(
        normed_rows,
        lax.all_gather(w_query[0], "seq", axis=0, tiled=True),
        preferred_element_type=jnp.float32,
    )
    keys = jnp.dot(
        normed,
        lax.all_gather(w_key[0], "seq", axis=0, tiled=True),
        preferred_element_type=jnp.float32,
    )
    values = jnp.dot(
        normed,
        lax.all_gather(w_value[0], "seq", axis=0, tiled=True),
        preferred_element_type=jnp.float32,
    )
    query = rotate(query.reshape(CAP, local_heads, HEAD_DIM), row_pos - row_start).astype(
        jnp.bfloat16
    )
    keys = rotate(keys.reshape(tokens, local_kv, HEAD_DIM), offsets).astype(jnp.bfloat16)
    values = values.reshape(tokens, local_kv, HEAD_DIM).astype(jnp.bfloat16)

    def masked_scores(query_rows, bounds, key_block, key_base):
        key_pos = key_base + jnp.arange(key_block.shape[0], dtype=jnp.int32)
        row_at = bounds[0][:, None]
        allowed = (key_pos[None, :] <= row_at) & (row_at - key_pos[None, :] < WINDOW)
        allowed = allowed & (key_pos[None, :] >= bounds[1][:, None])
        grouped = query_rows.reshape(CAP, local_kv, group, HEAD_DIM)
        scores = (
            jnp.einsum("cngd,knd->ngck", grouped, key_block, preferred_element_type=jnp.float32)
            * score_scale
        )
        return (jnp.where(allowed[None, None, :, :], scores, -1e30), allowed)

    reach = min(WINDOW // tokens, lax.axis_size("seq") - 1)
    own_scores, own_allowed = masked_scores(query, places, keys, base)
    row_peak, row_total = block_stats(own_scores, own_allowed)
    visited = []
    for step in range(1, reach + 1):
        guest = passed_along(query, "seq", -step)
        guest_places = passed_along(places, "seq", -step)
        guest_scores, guest_allowed = masked_scores(guest, guest_places, keys, base)
        guest_peak, guest_total = block_stats(guest_scores, guest_allowed)
        returned = passed_along(jnp.stack([guest_peak, guest_total]), "seq", step)
        back_peak = jnp.where(seq_index >= step, returned[0], -1e30)
        merged_peak = jnp.maximum(row_peak, back_peak)
        row_total = row_total * jnp.exp(row_peak - merged_peak) + returned[1] * jnp.exp(
            back_peak - merged_peak
        )
        row_peak = merged_peak
        visited.append(guest_scores)
    attended = weighted_values(own_scores, row_peak, row_total, values)
    for step in range(1, reach + 1):
        guest_stats = passed_along(jnp.stack([row_peak, row_total]), "seq", -step)
        share = weighted_values(visited[step - 1], guest_stats[0], guest_stats[1], values)
        attended = attended + passed_along(share, "seq", step)
    attended = attended.astype(jnp.bfloat16).reshape(CAP, query_cols)
    partial_out = jnp.dot(
        attended,
        lax.all_gather(w_out[0], "seq", axis=1, tiled=True),
        preferred_element_type=jnp.float32,
    )
    summed = lax.psum(partial_out, "tp")
    state = x_rows + summed
    final = rms_norm(state, final_gain[0]).astype(jnp.bfloat16)
    all_rows = lax.all_gather(final, "seq", axis=0, tiled=True)
    all_targets = lax.all_gather(row_target, "seq", axis=0, tiled=True)
    logits = jnp.dot(all_rows, head[0], preferred_element_type=jnp.float32)
    vocab_start = (seq_index * lax.axis_size("tp") + lax.axis_index("tp")) * head.shape[2]
    local_top = jnp.max(logits, axis=1)
    local_total = jnp.sum(jnp.exp(logits - local_top[:, None]), axis=1)
    hit = all_targets[:, None] == vocab_start + jnp.arange(head.shape[2], dtype=jnp.int32)[None, :]
    local_target = jnp.sum(jnp.where(hit, logits, 0.0), axis=1)
    merged_top, merged_total, merged_target = joined(
        (local_top, local_total, local_target), ("seq", "tp"), combine_stats
    )
    logp = merged_target - (merged_top + jnp.log(merged_total))
    own = lax.dynamic_slice_in_dim(logp, seq_index * CAP, CAP, 0)
    placed = jnp.sum(jnp.where(picks, own[:, None], 0.0), axis=0)
    return placed[None, :].astype(jnp.float32)


def place():
    return lax.axis_index("seq"), lax.axis_index("tp")


def greet(peers):
    barrier = pltpu.get_barrier_semaphore()
    for peer in peers:
        pl.semaphore_signal(barrier, inc=1, device_id=peer, device_id_type=pl.DeviceIdType.MESH)
    pl.semaphore_wait(barrier, len(peers))


def remote(source, target, send, recv, peer):
    return pltpu.make_async_remote_copy(
        src_ref=source,
        dst_ref=target,
        send_sem=send,
        recv_sem=recv,
        device_id=peer,
        device_id_type=pl.DeviceIdType.MESH,
    )


def everyone(seq, tp):
    s, t = place()
    return [
        ((d, e), {"seq": lax.rem(s + d, seq), "tp": lax.rem(t + e, tp)})
        for d in range(seq)
        for e in range(tp)
        if (d, e) != (0, 0)
    ]


def tell_all(seq, tp, value, out, send, recv):
    s, t = place()
    out[s, t] = value[...]
    copies = []
    for number, (_, peer) in enumerate(everyone(seq, tp)):
        copy = remote(value, out.at[s, t], send.at[number], recv.at[number], peer)
        copy.start()
        copies.append(copy)
    return copies


def project_kernel(
    seq,
    pick,
    big,
    meta,
    w_query,
    w_key,
    w_value,
    out,
    raw,
    told,
    half,
    blocks,
    parts,
    joins,
    send,
    recv,
    fsend,
    frecv,
    msend,
    mrecv,
    psend,
    precv,
    xsend,
    xrecv,
):
    s, t = place()
    other = 1 - t
    width = blocks.shape[-1]
    tokens = blocks.shape[2] - 2 * pick
    per = seq // 2
    greet([peer for _, peer in everyone(seq, 2)])
    beside = {"seq": s, "tp": other}
    first = remote(big.at[other], half, xsend, xrecv, beside)
    first.start()
    messages = tell_all(seq, 2, meta, told, msend, mrecv)

    def hand_out(base, view):
        for i in range(per):
            target = base * per + i

            @pl.when(target != s)
            def _():
                remote(
                    view(i),
                    blocks.at[s, t],
                    send.at[target],
                    recv.at[s],
                    {"seq": target, "tp": t},
                ).start()

            @pl.when(target == s)
            def _():
                remote(view(i), blocks.at[s, t], fsend.at[s], frecv.at[s], beside).start()
                blocks[s, t] = view(i)[...]

    own = lambda i: big.at[t, :, pl.ds(i * width, width)]
    got = lambda i: half.at[:, pl.ds(i * width, width)]
    hand_out(t, own)
    first.wait_recv()
    hand_out(other, got)

    def arrived(source):
        return remote(
            blocks.at[source, t], blocks.at[source, t], send.at[source], recv.at[source], beside
        )

    def passed(source):
        return remote(
            blocks.at[source, t], blocks.at[source, t], fsend.at[source], frecv.at[source], beside
        )

    side_of = s // 2
    partner = s + 1 - 2 * lax.rem(s, 2)
    toward = lax.rem(partner - s + seq, seq)

    def handed(chunk, kind):
        slot = (0, toward, 2, seq - toward)[kind]
        target = out.at[kind, chunk] if kind < 3 else joins.at[chunk]
        peer = lax.rem(s + 2, seq) if kind == 2 else partner
        return remote(
            parts.at[chunk, slot],
            target,
            psend.at[chunk, kind],
            precv.at[chunk, kind],
            {"seq": peer, "tp": t},
        )

    def combine(source):
        def one(side, carry):
            chunk = source * 2 + lax.rem(t + side, 2)
            handed(chunk, 3).wait_recv()
            both = parts[chunk, 2].astype(jnp.float32) + joins[chunk].astype(jnp.float32)
            parts[chunk, 2] = both.astype(jnp.bfloat16)
            handed(chunk, 2).start()
            return carry

        lax.fori_loop(0, 2, one, 0)

    def project(source, side):
        chunk = source * 2 + side
        rows = blocks[source, side, :tokens]
        chosen = blocks[source, side, tokens : tokens + pick]
        raw[source, side] = blocks[source, side, tokens + pick :]
        dot = functools.partial(jnp.dot, preferred_element_type=jnp.float32)
        for d in range(seq):
            target = lax.rem(s + d, seq)
            single = pl.ds(pl.multiple_of(target * HEAD_DIM, HEAD_DIM), HEAD_DIM)
            wide = out.shape[-1]
            double = pl.ds(pl.multiple_of(target * wide, wide), wide)
            place_at = out.at[0, chunk] if d == 0 else parts.at[chunk, d]
            place_at[:tokens, :HEAD_DIM] = dot(rows, w_key[:, single]).astype(jnp.bfloat16)
            place_at[:tokens, HEAD_DIM:] = dot(rows, w_value[:, single]).astype(jnp.bfloat16)
            place_at[tokens:] = dot(chosen, w_query[:, double]).astype(jnp.bfloat16)
        for kind in (3, 1):
            handed(chunk, kind).start()

    near, far = 2 - side_of, 3 * (1 - side_of)

    def choose(number, first, second, third, fourth):
        return jnp.where(
            number == 0,
            first,
            jnp.where(number == 1, second, jnp.where(number == 2, third, fourth)),
        )

    def step(number, carry):
        source = choose(number, s, partner, near, far)

        @pl.when(number > 0)
        def _():
            arrived(source).wait_recv()
            passed(source).start()

        def both(side, more):
            which = lax.rem(t + side, 2)

            @pl.when(side == 1)
            def _():
                passed(source).wait_recv()

            project(source, which)
            return more

        done = lax.fori_loop(0, 2, both, carry)

        @pl.when(number > 0)
        def _():
            combine(choose(number, s, partner, s, near))

        return done

    lax.fori_loop(0, seq, step, 0)
    combine(far)
    first.wait_send()
    for source in range(seq):

        @pl.when(source != s)
        def _():
            arrived(source).wait_send()

        passed(source).wait_send()
    for copy in messages:
        copy.wait()
    for chunk in range(2 * seq):
        for kind in (1, 2):
            handed(chunk, kind).wait()
        handed(chunk, 3).wait_send()


def project(big, meta, w_query, w_key, w_value, seq, pick):
    rows = big.shape[1]
    width = w_key.shape[0]
    wide = w_query.shape[1] // seq
    return pl.pallas_call(
        functools.partial(project_kernel, seq, pick),
        out_shape=(
            jax.ShapeDtypeStruct((3, 2 * seq, rows - pick, wide), jnp.bfloat16),
            jax.ShapeDtypeStruct((seq, 2, pick, width), jnp.bfloat16),
            jax.ShapeDtypeStruct((seq, 2) + meta.shape, jnp.float32),
        ),
        in_specs=[pl.BlockSpec(memory_space=pltpu.VMEM)] * 5,
        out_specs=[pl.BlockSpec(memory_space=pltpu.VMEM)] * 3,
        scratch_shapes=[
            pltpu.VMEM(big.shape[1:], jnp.bfloat16),
            pltpu.VMEM((seq, 2, rows, width), jnp.bfloat16),
            pltpu.VMEM((2 * seq, seq, rows - pick, wide), jnp.bfloat16),
            pltpu.VMEM((2 * seq, rows - pick, wide), jnp.bfloat16),
        ]
        + [pltpu.SemaphoreType.DMA((seq,))] * 4
        + [pltpu.SemaphoreType.DMA((2 * seq,))] * 2
        + [pltpu.SemaphoreType.DMA((2 * seq, seq))] * 2
        + [pltpu.SemaphoreType.DMA] * 2,
        compiler_params=pltpu.CompilerParams(collective_id=0, has_side_effects=True),
    )(big, meta, w_query, w_key, w_value)


def heads_kernel(seq, part, out, send, recv):
    s, t = place()
    width = part.shape[1]
    greet([{"seq": lax.rem(s + d, seq), "tp": t} for d in range(1, seq)])
    mine = pl.ds(pl.multiple_of(s * width, width), width)
    copies = []
    for d in range(1, seq):
        copy = remote(
            part, out.at[:, mine], send.at[d], recv.at[d], {"seq": lax.rem(s + d, seq), "tp": t}
        )
        copy.start()
        copies.append(copy)
    out[:, mine] = part[...]
    for copy in copies:
        copy.wait()


def gather_heads(part, seq):
    return pl.pallas_call(
        functools.partial(heads_kernel, seq),
        out_shape=jax.ShapeDtypeStruct((part.shape[0], part.shape[1] * seq), part.dtype),
        in_specs=[pl.BlockSpec(memory_space=pltpu.VMEM)],
        out_specs=pl.BlockSpec(memory_space=pltpu.VMEM),
        scratch_shapes=[pltpu.SemaphoreType.DMA((seq,))] * 2,
        compiler_params=pltpu.CompilerParams(collective_id=2, has_side_effects=True),
    )(part)


def rows_kernel(seq, part, squares, out, told, send, recv, fsend, frecv, msend, mrecv):
    s, t = place()
    rows, width = part.shape
    greet([peer for _, peer in everyone(seq, 2)])
    beside = {"seq": s, "tp": 1 - t}

    def spot(source, half):
        return out.at[
            pl.ds(pl.multiple_of(half * rows, rows), rows),
            pl.ds(pl.multiple_of(source * width, width), width),
        ]

    copies = []
    for d in (2, 1, 3)[: seq - 1]:
        copy = remote(part, spot(s, t), send.at[d], recv.at[d], {"seq": lax.rem(s + d, seq), "tp": t})
        copy.start()
        copies.append((d, copy))
    aside = remote(part, spot(s, t), fsend.at[0], frecv.at[0], beside)
    aside.start()
    forwards = [aside]
    messages = tell_all(seq, 2, squares, told, msend, mrecv)
    spot(s, t)[...] = part[...]
    for d, copy in copies[1:] + copies[:1]:
        copy.wait_recv()
        source = lax.rem(s - d + seq, seq)
        forward = remote(spot(source, t), spot(source, t), fsend.at[d], frecv.at[d], beside)
        forward.start()
        forwards.append(forward)
    for _, copy in copies:
        copy.wait_send()
    for copy in forwards + messages:
        copy.wait()


def gather_rows(part, squares, seq):
    rows, width = part.shape
    return pl.pallas_call(
        functools.partial(rows_kernel, seq),
        out_shape=(
            jax.ShapeDtypeStruct((2 * rows, width * seq), part.dtype),
            jax.ShapeDtypeStruct((seq, 2) + squares.shape, jnp.float32),
        ),
        in_specs=[pl.BlockSpec(memory_space=pltpu.VMEM)] * 2,
        out_specs=[pl.BlockSpec(memory_space=pltpu.VMEM)] * 2,
        scratch_shapes=[pltpu.SemaphoreType.DMA((seq,))] * 4
        + [pltpu.SemaphoreType.DMA((2 * seq,))] * 2,
        compiler_params=pltpu.CompilerParams(collective_id=3, has_side_effects=True),
    )(part, squares)


def stats_kernel(seq, stats, told, send, recv):
    greet([peer for _, peer in everyone(seq, 2)])
    for copy in tell_all(seq, 2, stats, told, send, recv):
        copy.wait()


def gather_stats(stats, seq):
    return pl.pallas_call(
        functools.partial(stats_kernel, seq),
        out_shape=jax.ShapeDtypeStruct((seq, 2) + stats.shape, jnp.float32),
        in_specs=[pl.BlockSpec(memory_space=pltpu.VMEM)],
        out_specs=pl.BlockSpec(memory_space=pltpu.VMEM),
        scratch_shapes=[pltpu.SemaphoreType.DMA((2 * seq,))] * 2,
        compiler_params=pltpu.CompilerParams(collective_id=4, has_side_effects=True),
    )(stats)


def padded(rows, lanes):
    stacked = jnp.stack([r.astype(jnp.float32) for r in rows])
    return jnp.pad(stacked, ((0, 8 - len(rows)), (0, lanes - stacked.shape[1])))


def picks_of(mask):
    ranking = jnp.cumsum(mask, axis=-1) - 1
    return (mask[..., None, :] == 1) & (
        ranking[..., None, :] == jnp.arange(CAP, dtype=jnp.int32)[:, None]
    )


def moved_rows(
    hidden,
    segment_ids,
    targets,
    loss_mask,
    attn_gain,
    final_gain,
    w_query,
    w_key,
    w_value,
    w_out,
    head,
):
    seq = lax.axis_size("seq")
    s, t = place()
    tokens, features = hidden.shape[1:]
    model = features * 2
    width = w_key.shape[1]
    length = seq * tokens
    x = hidden[0]
    xfloat = x.astype(jnp.float32)
    gain = lax.dynamic_slice_in_dim(attn_gain[0], t * features, features)
    scaled = (xfloat * gain).astype(jnp.bfloat16)
    squares = jnp.sum(xfloat * xfloat, axis=1)
    chooser = picks_of(loss_mask).astype(jnp.bfloat16)
    pick_scaled = jnp.dot(chooser, scaled, preferred_element_type=jnp.float32).astype(jnp.bfloat16)
    pick_raw = jnp.dot(chooser, x, preferred_element_type=jnp.float32).astype(jnp.bfloat16)
    big = jnp.concatenate(
        [
            scaled.reshape(2, tokens // 2, features),
            pick_scaled.reshape(2, CAP // 2, features),
            pick_raw.reshape(2, CAP // 2, features),
        ],
        axis=1,
    )
    meta = padded([segment_ids, loss_mask, targets, squares], tokens)
    parts, raw, told = project(big, meta, w_query[0], w_key[0], w_value[0], seq, CAP // 2)
    half = tokens // 2
    raw_block = raw.reshape(seq * CAP, width)

    whole = told[:, 0].astype(jnp.int32)
    segments = whole[:, 0].reshape(length)
    masks = whole[:, 1]
    position = jnp.arange(length, dtype=jnp.int32)
    member = segments[None, :] == jnp.arange(SEGMENTS, dtype=jnp.int32)[:, None]
    starts = jnp.min(jnp.where(member, position[None, :], FARTHEST), axis=1)
    token_start = jnp.sum(jnp.where(member, starts[:, None], 0), axis=0)
    offsets = position - token_start
    scale = lax.rsqrt((told[:, 0, 3] + told[:, 1, 3]) / model + EPS)
    picks = picks_of(masks)

    def chosen(values):
        return jnp.sum(jnp.where(picks, values.reshape(seq, 1, tokens), 0), axis=2).reshape(-1)

    row_pos = chosen(position)
    row_start = chosen(token_start)
    row_target = chosen(whole[:, 2])
    row_scale = chosen(scale)

    summed = jnp.sum(parts.astype(jnp.float32), axis=0)
    key_all = summed[:, :half, :HEAD_DIM].reshape(length, HEAD_DIM) * scale.reshape(length, 1)
    value_all = summed[:, :half, HEAD_DIM:].reshape(length, HEAD_DIM) * scale.reshape(length, 1)
    value_all = value_all.astype(jnp.bfloat16)
    query_all = summed[:, half:].reshape(seq * CAP, -1) * row_scale[:, None]
    group = query_all.shape[1] // HEAD_DIM
    key_all = rotate(key_all[:, None, :], offsets)[:, 0].astype(jnp.bfloat16)
    query_all = rotate(query_all.reshape(seq * CAP, group, HEAD_DIM), row_pos - row_start).astype(
        jnp.bfloat16
    )
    allowed = (position[None, :] <= row_pos[:, None]) & (position[None, :] >= row_start[:, None])
    allowed = allowed & (row_pos[:, None] - position[None, :] < WINDOW)
    scores = jnp.einsum("cgd,kd->gck", query_all, key_all, preferred_element_type=jnp.float32)
    scores = jnp.where(allowed[None], scores * HEAD_DIM ** (-0.5), -1e30)
    peak = jnp.max(scores, axis=-1, keepdims=True)
    lifted = jnp.exp(scores - peak)
    weights = (lifted / jnp.sum(lifted, axis=-1, keepdims=True)).astype(jnp.bfloat16)
    attended = jnp.einsum("gck,kd->cgd", weights, value_all, preferred_element_type=jnp.float32)
    attended = attended.astype(jnp.bfloat16).reshape(seq * CAP, group * HEAD_DIM)
    attended = gather_heads(attended, seq)
    partial_out = jnp.dot(attended, w_out[0], preferred_element_type=jnp.float32)

    rows = seq * CAP // 2
    away = lax.dynamic_slice_in_dim(partial_out, (1 - t) * rows, rows).astype(jnp.bfloat16)
    here = lax.dynamic_slice_in_dim(partial_out, t * rows, rows)
    here = here + lax.dynamic_slice_in_dim(raw_block, t * rows, rows).astype(jnp.float32)
    state = here + lax.ppermute(away, "tp", [(0, 1), (1, 0)]).astype(jnp.float32)
    late_gain = lax.dynamic_slice_in_dim(final_gain[0], s * width, width)
    late = (state * late_gain).astype(jnp.bfloat16)
    final, late_squares = gather_rows(late, padded([jnp.sum(state * state, axis=1)], 128), seq)
    late_mean = jnp.sum(late_squares[:, :, 0, :rows], axis=0).reshape(-1) / model
    logits = jnp.dot(final, head[0], preferred_element_type=jnp.float32)
    logits = logits * lax.rsqrt(late_mean + EPS)[:, None]
    entries = head.shape[2]
    first_entry = (s * 2 + t) * entries
    top = jnp.max(logits, axis=1)
    exps = jnp.sum(jnp.exp(logits - top[:, None]), axis=1)
    hit = row_target[:, None] == first_entry + jnp.arange(entries, dtype=jnp.int32)[None, :]
    found = jnp.sum(jnp.where(hit, logits, 0.0), axis=1)
    stats = gather_stats(padded([top, exps, found], seq * CAP), seq)
    mine = lax.dynamic_slice_in_dim(stats.reshape(seq * 2, 8, seq * CAP), s * CAP, CAP, 2)
    best = jnp.max(mine[:, 0], axis=0)
    summed = jnp.sum(mine[:, 1] * jnp.exp(mine[:, 0] - best[None, :]), axis=0)
    logp = jnp.sum(mine[:, 2], axis=0) - (best + jnp.log(summed))
    placed = jnp.sum(jnp.where(picks_of(loss_mask), logp[:, None], 0.0), axis=0)
    return placed[None, :].astype(jnp.float32)


def solution(mesh):
    placed = (
        P("ref", ("groups", "seq"), "tp"),
        P(("groups", "seq")),
        P(("groups", "seq")),
        P(("groups", "seq")),
        P("ref", None),
        P("ref", None),
        P("ref", "seq", "tp"),
        P("ref", "seq", "tp"),
        P("ref", "seq", "tp"),
        P("ref", "tp", "seq"),
        P("ref", None, ("seq", "tp")),
    )

    def shards(*args):
        seq, tp = mesh.shape["seq"], mesh.shape["tp"]
        own_heads = args[7].shape[2] // HEAD_DIM
        moves = tp == 2 and seq == 4 and own_heads == seq and args[6].shape[2] == 2 * args[7].shape[2]
        return (moved_rows if moves else gathered_weights)(*args)

    return jax.shard_map(
        shards, mesh=mesh, in_specs=placed, out_specs=P("ref", ("groups", "seq")), check_vma=False
    )
```

profile of v0, /device:TPU:0, one launch (start us, length us, event | category | flops | bytes accessed | tf_op | source)
XLA Modules:
  0.0 164.3 jit_solution(2311115626063322874)
XLA Ops:
  0.0 0.0 copy-start
  0.0 0.8 broadcast_compare_fusion.1
  0.8 0.7 convert_element_type.99
  1.6 1.0 reduce-window.15
  2.6 0.1 slice.65
  2.7 0.1 slice_reduce_fusion.1
  2.8 0.1 add_bitcast_fusion.1
  2.9 1.5 fusion.4
  4.4 0.7 constant_dynamic-slice_fusion.3
  5.1 1.5 convolution_convert_fusion
  6.6 0.0 copy-done.1
  6.6 0.3 convolution_convert_fusion.1
  6.9 0.2 fusion.5
  7.2 0.0 copy-done.3
  7.2 0.0 copy-done.4
  7.2 1.1 pad_maximum_fusion.big
  8.4 0.6 select_maximum_fusion.meta
  9.0 84.9 %shard_map.109 = (bf16[3,8,144,256]{3,2,1,0:T(8,128)(2,1)}, bf16[4,2,16,1024]{3,2,1,0:T(8,128)(2,1)}, f32[4,2,8,256]{3,2,1,0:T(8,128)}) custom-call(bf16[2,160,2048]{2,1,0:T(8,128)(2,1)} %pad_maximum_fusion.big, f32[8,256]{1,0:T(8,128)} %select_maximum_fusion.meta, bf16[1024,1024]{1,0:T(8,128)(2,1)} %bitcast.94, bf16[1024,512]{1,0:T(8,128)(2,1)} %bitcast.97, ...), custom_call_target="tpu_custom_call" | custom-call | tf_op jit(solution)/shard_map/pallas_call | solution.py:414
  93.8 0.8 convert_bitcast_fusion
  94.7 0.8 add_rsqrt_fusion
  95.5 0.1 select_reduce_fusion.7
  95.6 0.1 select_reduce_fusion.6
  95.7 1.9 %convert_reduce_fusion = f32[8,144,256]{2,1,0:T(8,128)S(1)} fusion(bf16[3,8,144,256]{3,2,1,0:T(8,128)(2,1)} %get-tuple-element.10), kind=kLoop, calls=%fused_computation.3 | loop fusion | flops 1474560 | bytes 2949120 | tf_op jit(solution)/shard_map/reduce_sum | solution.py:603
  97.6 0.9 fusion.48
  98.5 1.2 reduce-window.19
  99.7 0.1 slice.88
  99.8 0.1 copy.33
  99.9 0.1 copy.34
  100.0 0.1 add_bitcast_fusion
  100.1 0.3 select_reduce_fusion.1
  100.4 0.1 ge.17
  100.5 0.1 le.24
  100.6 0.2 fusion.20
  100.8 0.1 select_reduce_fusion.2
  100.9 0.1 mul.212
  101.0 0.1 reshape.450
  101.0 1.2 copy.43
  102.3 0.3 multiply_cosine_fusion.1
  102.6 0.1 copy_multiply_fusion
  102.7 1.2 fusion.26
  103.9 0.1 subtract_convert_fusion
  104.0 1.4 fusion.11
  105.4 0.7 fusion.50
  106.1 0.2 copy.32
  106.3 2.0 %convolution_convert_fusion.2 = bf16[128,2,128]{2,0,1:T(8,128)(2,1)S(1)} fusion(f32[2,128]{1,0:T(2,128)S(1)} %fusion.50, f32[1024,128]{0,1:T(8,128)S(1)} %copy.32, f32[1024]{0:T(1024)S(1)} %bitcast.107, f32[2,128,1024]{1,2,0:T(8,128)} %fusion.11), kind=kOutput, calls=%fused_computation.21 | convolution fusion | flops 68191488 | bytes 1643520 | tf_op jit(solution)/shard_map/gck,kd->cgd/dot_general | solution.py:620
  108.3 0.0 copy-start.2
  108.3 0.7 copy.45.part
  109.1 12.0 %shard_map.110 = bf16[128,1024]{1,0:T(8,128)(2,1)} custom-call(bf16[128,256]{1,0:T(8,128)(2,1)} %copy.45.part), custom_call_target="tpu_custom_call" | custom-call | tf_op jit(solution)/shard_map/pallas_call | solution.py:455
  121.0 1.4 fusion.6
  122.5 0.1 collective-permute-start
  122.6 0.1 eq.87
  122.7 0.7 constant_dynamic-slice_fusion.1
  123.3 4.2 %collective-permute-done = bf16[64,1024]{1,0:T(8,128)(2,1)S(1)} collective-permute-done((bf16[64,1024]{1,0:T(8,128)(2,1)S(1)}, bf16[64,1024]{1,0:T(8,128)(2,1)S(1)}, u32[]{:S(2)}, u32[]{:S(2)}) %collective-permute-start) | collective-permute-done | bytes 131104 | tf_op jit(solution)/shard_map/ppermute | solution.py:629
  127.5 0.8 multiply_reduce_fusion
  128.3 0.6 pad.13.squares
  128.9 19.0 %shard_map.111 = (bf16[128,4096]{1,0:T(8,128)(2,1)}, f32[4,2,8,128]{3,2,1,0:T(8,128)}) custom-call(bf16[64,1024]{1,0:T(8,128)(2,1)} %get-tuple-element.23.part, f32[8,128]{1,0:T(8,128)} %pad.13.squares), custom_call_target="tpu_custom_call" | custom-call | tf_op jit(solution)/shard_map/pallas_call | solution.py:501
  147.9 0.8 slice_reduce_fusion
  148.7 0.1 rsqrt.31
  148.8 3.3 %fusion.51 = (f32[128]{0:T(128)S(1)}, f32[128,512]{1,0:T(8,128)S(1)}) fusion(f32[128]{0:T(128)S(1)} %rsqrt.31, bf16[128,4096]{1,0:T(8,128)(2,1)} %get-tuple-element.13, bf16[1,4096,512]{2,1,0:T(8,128)(2,1)} %param.21), kind=kOutput, calls=%fused_computation.116 | convolution fusion | flops 537001856 | bytes 5506048 | tf_op jit(solution)/shard_map/dot_general | solution.py:634
  152.1 0.2 exponential_reduce_fusion
  152.3 0.6 select_maximum_fusion.3.stats
  152.9 9.7 %shard_map.112 = f32[4,2,8,128]{3,2,1,0:T(8,128)} custom-call(f32[8,128]{1,0:T(8,128)} %select_maximum_fusion.3.stats), custom_call_target="tpu_custom_call" | custom-call | tf_op jit(solution)/shard_map/pallas_call | solution.py:522
  162.6 1.0 constant_dynamic-slice_fusion
  163.7 0.7 select_reduce_fusion.5
  (29 shorter events, 0.3 us)
Async XLA Ops:
  0.0 121.0 %copy-start = (bf16[1,1024,1024]{2,1,0:T(8,128)(2,1)S(1)}, bf16[1,1024,1024]{2,1,0:T(8,128)(2,1)}, u32[]{:S(2)}) copy-start(bf16[1,1024,1024]{2,1,0:T(8,128)(2,1)} %param.20) | copy-start | bytes 6291460
  0.0 6.6 %copy-start.1 = (bf16[1,256,2048]{2,1,0:T(8,128)(2,1)S(1)}, bf16[1,256,2048]{2,1,0:T(8,128)(2,1)}, u32[]{:S(2)}) copy-start(bf16[1,256,2048]{2,1,0:T(8,128)(2,1)} %param.11) | copy-start | bytes 3145732
  5.1 2.1 %copy-start.3 = (s32[256]{0:T(256)S(1)}, s32[256]{0:T(256)}, u32[]{:S(2)}) copy-start(s32[256]{0:T(256)} %param.12) | copy-start | bytes 3076
  5.1 2.1 %copy-start.4 = (s32[256]{0:T(256)S(1)}, s32[256]{0:T(256)}, u32[]{:S(2)}) copy-start(s32[256]{0:T(256)} %param.13) | copy-start | bytes 3076
  108.3 19.2 %copy-start.2 = (bf16[4,2,16,1024]{3,2,1,0:T(8,128)(2,1)S(1)}, bf16[4,2,16,1024]{3,2,1,0:T(8,128)(2,1)}, u32[]{:S(2)}) copy-start(bf16[4,2,16,1024]{3,2,1,0:T(8,128)(2,1)} %get-tuple-element.12) | copy-start | bytes 786436
  122.5 5.0 %collective-permute-start = (bf16[64,1024]{1,0:T(8,128)(2,1)S(1)}, bf16[64,1024]{1,0:T(8,128)(2,1)S(1)}, u32[]{:S(2)}, u32[]{:S(2)}) collective-permute-start(bf16[64,1024]{1,0:T(8,128)(2,1)S(1)} %dynamic-slice_convert_fusion), channel_id=1, source_target_pairs={{0,2},{2,0},{1,3},{3,1},{4,6},{6,4},{5,7},{7,5},{8,10},{10,8},{9,1... | collective-permute-start | bytes 393224 | tf_op jit(solution)/shard_map/ppermute | solution.py:629
where the time goes:
time: 165 us; the launch traced here: 164 us
  Pallas kernels  126 us (76%)
  other arithmetic  17.6 us (11%)
  matrix products  10.6 us (6%)
  local copies, waits for them, and re-layouts  6.1 us (4%)
  waiting for transfers between devices  4.16 us (3%)
    pallas_call x1, Pallas kernels, project(): pl.pallas_call(functools.partial(project_kernel, seq, pick), out_shape=(j...  84.9 us
    pallas_call x1, Pallas kernels, gather_rows(): pl.pallas_call(functools.partial(rows_kernel, seq), out_shape=(jax.ShapeD...  19 us
    pallas_call x1, Pallas kernels, gather_heads(): pl.pallas_call(functools.partial(heads_kernel, seq), out_shape=jax.ShapeD...  12 us
    pallas_call x1, Pallas kernels, gather_stats(): pl.pallas_call(functools.partial(stats_kernel, seq), out_shape=jax.ShapeD...  9.7 us
    ppermute x1, waiting for transfers between devices, moved_rows(): lax.ppermute(away, 'tp', [(0, 1), (1, 0)]).astype(jnp.float32)  4.16 us
    another operation x6, other arithmetic  3.52 us
    dot_general x1, matrix products, moved_rows(): logits = jnp.dot(final, head[0], preferred_element_type=jnp.float32)  3.31 us
  transfers between devices with their start and end apart: 1, of which 1 were waited for; matrix products, arithmetic and copies ran while one was open for 0% of the time, Pallas kernels for 0%

commit v1 on v0

v1 whole, which is shorter than its diff:
```python
import functools

import jax
import jax.numpy as jnp
import numpy as np
from jax import lax
from jax.experimental import pallas as pl
from jax.experimental.pallas import tpu as pltpu
from jax.sharding import PartitionSpec as P

HEAD_DIM = 128
WINDOW = 2048
CAP = 32
SEGMENTS = 4


EPS = 1e-05
THETA = 500000.0
FARTHEST = 1073741824


def passed_along(value, axis, by):
    length = lax.axis_size(axis)
    pairs = [(i, i + by) for i in range(length) if 0 <= i + by < length]
    return lax.ppermute(value, axis, pairs)


def joined(part, axis, combine):
    gathered = jax.tree.map(lambda a: lax.all_gather(a, axis), part)

    def take(source):
        return jax.tree.map(lambda a: lax.dynamic_index_in_dim(a, source, 0, False), gathered)

    return lax.fori_loop(
        1, lax.axis_size(axis), lambda source, state: combine(state, take(source)), take(0)
    )


def rms_norm(values, gain):
    return values * lax.rsqrt(jnp.mean(values * values, axis=-1, keepdims=True) + EPS) * gain


def rotate(tensor, offsets):
    half = tensor.shape[-1] // 2
    freq = THETA ** (-(jnp.arange(half, dtype=jnp.float32) * 2.0 / tensor.shape[-1]))
    angle = offsets.astype(jnp.float32)[:, None] * freq[None, :]
    cosine = jnp.cos(angle)[:, None, :]
    sine = jnp.sin(angle)[:, None, :]
    first = tensor[..., :half]
    second = tensor[..., half:]
    return jnp.concatenate(
        [first * cosine - second * sine, second * cosine + first * sine], axis=-1
    )


def combine_stats(left, right):
    top = jnp.maximum(left[0], right[0])
    total = left[1] * jnp.exp(left[0] - top) + right[1] * jnp.exp(right[0] - top)
    return (top, total, left[2] + right[2])


def block_stats(scores, allowed):
    row_peak = jnp.max(scores, axis=-1)
    lifted = jnp.where(allowed[None, None, :, :], jnp.exp(scores - row_peak[..., None]), 0.0)
    return (row_peak, jnp.sum(lifted, axis=-1))


def weighted_values(scores, row_peak, row_total, value_block):
    safe_total = jnp.where(row_total > 0.0, row_total, 1.0)
    weights = (jnp.exp(scores - row_peak[..., None]) / safe_total[..., None]).astype(jnp.bfloat16)
    return jnp.einsum("ngck,knd->cngd", weights, value_block, preferred_element_type=jnp.float32)


def gathered_weights(
    hidden,
    segment_ids,
    targets,
    loss_mask,
    attn_gain,
    final_gain,
    w_query,
    w_key,
    w_value,
    w_out,
    head,
):
    tokens = hidden.shape[1]
    seq_index = lax.axis_index("seq")
    base = seq_index * tokens
    position = base + jnp.arange(tokens, dtype=jnp.int32)
    whole = lax.all_gather(hidden[0], "tp", axis=1, tiled=True)
    xfloat = whole.astype(jnp.float32)
    normed = rms_norm(xfloat, attn_gain[0]).astype(jnp.bfloat16)
    labels = jnp.arange(SEGMENTS, dtype=jnp.int32)
    member = segment_ids[None, :] == labels[:, None]
    local_first = jnp.min(jnp.where(member, position[None, :], FARTHEST), axis=1)
    starts = lax.pmin(local_first, "seq")
    token_start = jnp.sum(jnp.where(member, starts[:, None], 0), axis=0)
    offsets = position - token_start
    ranking = jnp.cumsum(loss_mask) - 1
    picks = (loss_mask[None, :] == 1) & (
        ranking[None, :] == jnp.arange(CAP, dtype=jnp.int32)[:, None]
    )
    chooser = picks.astype(jnp.bfloat16)
    normed_rows = jnp.dot(chooser, normed, preferred_element_type=jnp.float32).astype(jnp.bfloat16)
    x_rows = jnp.dot(chooser, whole, preferred_element_type=jnp.float32)
    row_pos = jnp.sum(jnp.where(picks, position[None, :], 0), axis=1)
    row_start = jnp.sum(jnp.where(picks, token_start[None, :], 0), axis=1)
    row_target = jnp.sum(jnp.where(picks, targets[None, :], 0), axis=1)
    places = jnp.stack([row_pos, row_start])
    query_cols = w_query.shape[2]
    key_cols = w_key.shape[2]
    local_heads = query_cols // HEAD_DIM
    local_kv = key_cols // HEAD_DIM
    group = local_heads // local_kv
    score_scale = HEAD_DIM ** (-0.5)
    query = jnp.dot(
        normed_rows,
        lax.all_gather(w_query[0], "seq", axis=0, tiled=True),
        preferred_element_type=jnp.float32,
    )
    keys = jnp.dot(
        normed,
        lax.all_gather(w_key[0], "seq", axis=0, tiled=True),
        preferred_element_type=jnp.float32,
    )
    values = jnp.dot(
        normed,
        lax.all_gather(w_value[0], "seq", axis=0, tiled=True),
        preferred_element_type=jnp.float32,
    )
    query = rotate(query.reshape(CAP, local_heads, HEAD_DIM), row_pos - row_start).astype(
        jnp.bfloat16
    )
    keys = rotate(keys.reshape(tokens, local_kv, HEAD_DIM), offsets).astype(jnp.bfloat16)
    values = values.reshape(tokens, local_kv, HEAD_DIM).astype(jnp.bfloat16)

    def masked_scores(query_rows, bounds, key_block, key_base):
        key_pos = key_base + jnp.arange(key_block.shape[0], dtype=jnp.int32)
        row_at = bounds[0][:, None]
        allowed = (key_pos[None, :] <= row_at) & (row_at - key_pos[None, :] < WINDOW)
        allowed = allowed & (key_pos[None, :] >= bounds[1][:, None])
        grouped = query_rows.reshape(CAP, local_kv, group, HEAD_DIM)
        scores = (
            jnp.einsum("cngd,knd->ngck", grouped, key_block, preferred_element_type=jnp.float32)
            * score_scale
        )
        return (jnp.where(allowed[None, None, :, :], scores, -1e30), allowed)

    reach = min(WINDOW // tokens, lax.axis_size("seq") - 1)
    own_scores, own_allowed = masked_scores(query, places, keys, base)
    row_peak, row_total = block_stats(own_scores, own_allowed)
    visited = []
    for step in range(1, reach + 1):
        guest = passed_along(query, "seq", -step)
        guest_places = passed_along(places, "seq", -step)
        guest_scores, guest_allowed = masked_scores(guest, guest_places, keys, base)
        guest_peak, guest_total = block_stats(guest_scores, guest_allowed)
        returned = passed_along(jnp.stack([guest_peak, guest_total]), "seq", step)
        back_peak = jnp.where(seq_index >= step, returned[0], -1e30)
        merged_peak = jnp.maximum(row_peak, back_peak)
        row_total = row_total * jnp.exp(row_peak - merged_peak) + returned[1] * jnp.exp(
            back_peak - merged_peak
        )
        row_peak = merged_peak
        visited.append(guest_scores)
    attended = weighted_values(own_scores, row_peak, row_total, values)
    for step in range(1, reach + 1):
        guest_stats = passed_along(jnp.stack([row_peak, row_total]), "seq", -step)
        share = weighted_values(visited[step - 1], guest_stats[0], guest_stats[1], values)
        attended = attended + passed_along(share, "seq", step)
    attended = attended.astype(jnp.bfloat16).reshape(CAP, query_cols)
    partial_out = jnp.dot(
        attended,
        lax.all_gather(w_out[0], "seq", axis=1, tiled=True),
        preferred_element_type=jnp.float32,
    )
    summed = lax.psum(partial_out, "tp")
    state = x_rows + summed
    final = rms_norm(state, final_gain[0]).astype(jnp.bfloat16)
    all_rows = lax.all_gather(final, "seq", axis=0, tiled=True)
    all_targets = lax.all_gather(row_target, "seq", axis=0, tiled=True)
    logits = jnp.dot(all_rows, head[0], preferred_element_type=jnp.float32)
    vocab_start = (seq_index * lax.axis_size("tp") + lax.axis_index("tp")) * head.shape[2]
    local_top = jnp.max(logits, axis=1)
    local_total = jnp.sum(jnp.exp(logits - local_top[:, None]), axis=1)
    hit = all_targets[:, None] == vocab_start + jnp.arange(head.shape[2], dtype=jnp.int32)[None, :]
    local_target = jnp.sum(jnp.where(hit, logits, 0.0), axis=1)
    merged_top, merged_total, merged_target = joined(
        (local_top, local_total, local_target), ("seq", "tp"), combine_stats
    )
    logp = merged_target - (merged_top + jnp.log(merged_total))
    own = lax.dynamic_slice_in_dim(logp, seq_index * CAP, CAP, 0)
    placed = jnp.sum(jnp.where(picks, own[:, None], 0.0), axis=0)
    return placed[None, :].astype(jnp.float32)


def place():
    return lax.axis_index("seq"), lax.axis_index("tp")


def greet(peers):
    barrier = pltpu.get_barrier_semaphore()
    for peer in peers:
        pl.semaphore_signal(barrier, inc=1, device_id=peer, device_id_type=pl.DeviceIdType.MESH)
    pl.semaphore_wait(barrier, len(peers))


def remote(source, target, send, recv, peer):
    return pltpu.make_async_remote_copy(
        src_ref=source,
        dst_ref=target,
        send_sem=send,
        recv_sem=recv,
        device_id=peer,
        device_id_type=pl.DeviceIdType.MESH,
    )


def everyone(seq, tp):
    s, t = place()
    return [
        ((d, e), {"seq": lax.rem(s + d, seq), "tp": lax.rem(t + e, tp)})
        for d in range(seq)
        for e in range(tp)
        if (d, e) != (0, 0)
    ]


def tell_all(seq, tp, value, out, send, recv):
    s, t = place()
    out[s, t] = value[...]
    copies = []
    for number, (_, peer) in enumerate(everyone(seq, tp)):
        copy = remote(value, out.at[s, t], send.at[number], recv.at[number], peer)
        copy.start()
        copies.append(copy)
    return copies


def fused_kernel(
    seq,
    x,
    segs,
    mask,
    target_ids,
    freq,
    attn_gain,
    final_gain,
    wq_hbm,
    wk_hbm,
    wv_hbm,
    wo_hbm,
    head_hbm,
    out,
    wq,
    wk,
    wv,
    wo,
    head,
    meta,
    told,
    half,
    blocks,
    parts,
    inbox,
    qparts,
    qinbox,
    picks,
    rowinfo,
    scales,
    tables,
    keys,
    values,
    queries,
    att,
    rawrows,
    away,
    arrived_away,
    here,
    fin,
    logits,
    squares,
    sqtold,
    stats,
    sttold,
    wsem,
    xsend,
    xrecv,
    send,
    recv,
    fsend,
    frecv,
    msend,
    mrecv,
    csend,
    crecv,
    qsend,
    qrecv,
    asend,
    arecv,
    esend,
    erecv,
    zsend,
    zrecv,
    bsend,
    brecv,
    sqsend,
    sqrecv,
    stsend,
    strecv,
):
    f32, bf16 = jnp.float32, jnp.bfloat16
    s, t = place()
    other = 1 - t
    side = s // 2
    is_end = jnp.logical_or(s == 0, s == seq - 1)
    is_mid = jnp.logical_not(is_end)
    home = side == t
    tokens = x.shape[0]
    model = x.shape[1] * 2
    rows = tokens // 4
    width = model // seq
    beside = {"seq": s, "tp": other}
    dot = functools.partial(jnp.dot, preferred_element_type=f32)

    loads = [
        pltpu.make_async_copy(a, b, wsem.at[i])
        for i, (a, b) in enumerate(
            ((wk_hbm, wk), (wv_hbm, wv), (wq_hbm, wq), (wo_hbm, wo), (head_hbm, head))
        )
    ]
    for load in loads:
        load.start()
    greet([peer for _, peer in everyone(seq, 2)])

    def piece(which, p, i):
        at = pl.multiple_of((which * 2 + p) * rows, rows)
        return x.at[pl.ds(at, rows), pl.ds(i * width, width)]

    def got(p, i):
        return half.at[p, :, pl.ds(i * width, width)]

    pairs = [(p, i) for p in range(2) for i in range(2)]
    firsts = {
        (p, i): remote(piece(other, p, i), got(p, i), xsend.at[p, i], xrecv.at[p, i], beside)
        for p, i in pairs
    }
    for pair in pairs:
        firsts[pair].start()

    def arrived(source, p):
        block = blocks.at[source, t * 2 + p]
        return remote(block, block, send.at[source, p], recv.at[source, p], beside)

    def passed(source, p):
        block = blocks.at[source, t * 2 + p]
        return remote(block, block, fsend.at[source, p], frecv.at[source, p], beside)

    def hand(view, target, p):
        remote(
            view, blocks.at[s, t * 2 + p], send.at[target, p], recv.at[s, p], {"seq": target, "tp": t}
        ).start()

    for p, i in pairs:
        target = t * 2 + i

        @pl.when(target != s)
        def _():
            hand(piece(t, p, i), target, p)

        @pl.when(target == s)
        def _():
            remote(
                piece(t, p, i), blocks.at[s, t * 2 + p], fsend.at[s, p], frecv.at[s, p], beside
            ).start()
            blocks[s, t * 2 + p] = piece(t, p, i)[...]
            blocks[s, other * 2 + p] = piece(other, p, i)[...]

    fold = jnp.zeros((tokens, 128), f32)
    for c in range(x.shape[1] // 128):
        part = x[:, c * 128 : (c + 1) * 128].astype(f32)
        fold = fold + part * part
    meta[0:1, :] = segs[...].astype(f32)
    meta[1:2, :] = mask[...].astype(f32)
    meta[2:3, :] = target_ids[...].astype(f32)
    meta[3:4, :] = jnp.sum(fold.T, axis=0, keepdims=True)
    meta[4:8, :] = jnp.zeros((4, tokens), f32)
    messages = tell_all(seq, 2, meta, told, msend, mrecv)

    for p, i in pairs:
        firsts[p, i].wait_recv()
        target = other * 2 + i

        @pl.when(target != s)
        def _():
            hand(got(p, i), target, p)

        @pl.when(target == s)
        def _():
            blocks[s, t * 2 + p] = got(p, i)[...]

    for message in messages:
        message.wait_recv()

    upper = lax.broadcasted_iota(jnp.int32, (tokens, tokens), 0)
    upper = (upper <= lax.broadcasted_iota(jnp.int32, (tokens, tokens), 1)).astype(f32).astype(bf16)
    spot = lax.broadcasted_iota(jnp.int32, (1, tokens), 1).astype(f32)
    order = lax.broadcasted_iota(jnp.int32, (CAP, tokens), 0).astype(f32) + 1.0
    begins = [jnp.full((1, 1), float(FARTHEST), f32) for _ in range(SEGMENTS)]
    for b in range(seq):
        seg = told[b, 0, 0:1, :]
        for j in range(SEGMENTS):
            low = jnp.where(seg == float(j), spot + float(b * tokens), float(FARTHEST))
            begins[j] = jnp.minimum(begins[j], jnp.min(low, axis=1, keepdims=True))
    for b in range(seq):
        chosen = told[b, 0, 1:2, :]
        rank = dot(jnp.broadcast_to(chosen, (8, tokens)).astype(bf16), upper)[0:1, :]
        hit = jnp.logical_and(chosen == 1.0, rank == order)
        picks[b] = jnp.where(hit, 1.0, 0.0).astype(bf16)

        def column(line):
            return jnp.sum(jnp.where(hit, line, 0.0), axis=1, keepdims=True)

        scale = lax.rsqrt((told[b, 0, 3:4, :] + told[b, 1, 3:4, :]) / model + EPS)
        scales[0:1, b * tokens : (b + 1) * tokens] = scale
        seg = column(told[b, 0, 0:1, :])
        begin = jnp.zeros((CAP, 1), f32)
        for j in range(SEGMENTS):
            begin = begin + jnp.where(seg == float(j), begins[j], 0.0)
        here_rows = slice(b * CAP, (b + 1) * CAP)
        info = (column(spot + float(b * tokens)), begin, column(told[b, 0, 2:3, :]), column(scale))
        for kind, value in enumerate(info):
            rowinfo[kind, here_rows] = jnp.broadcast_to(value, (CAP, 128))

    gain = attn_gain[0:1, pl.ds(pl.multiple_of(s * width, width), width)]
    for load in loads[:3]:
        load.wait()
    kcols = wk.shape[1] // 2
    qcols = wq.shape[1] // 2
    partner = s + 1 - 2 * lax.rem(s, 2)
    near, far = 2 - side, 3 * (1 - side)

    def choose(number, options):
        value = options[-1]
        for k in range(len(options) - 2, -1, -1):
            value = jnp.where(number == k, options[k], value)
        return value

    def pick_from(number, codes):
        code = choose(number, codes)
        return choose(code // 4, (s, partner, near, far)), jnp.where(
            lax.rem(code, 4) < 2, t * 2 + lax.rem(code, 4), other * 2 + lax.rem(code, 4) - 2
        ), lax.rem(code, 4)

    def tok_ship(d, source, g):
        peer = {"seq": lax.rem(s + 2 * d - 1 + seq, seq), "tp": t}
        chunk = source * 4 + g
        return remote(
            parts.at[d, chunk], inbox.at[d, chunk], csend.at[d, chunk], crecv.at[d, chunk], peer
        )

    def que_ship(d, source):
        peer = {"seq": lax.rem(s + 2 * d - 1 + seq, seq), "tp": t}
        return remote(
            qparts.at[d, source], qinbox.at[d, source], qsend.at[d, source], qrecv.at[d, source], peer
        )

    def ship(d, source, g, last):
        tok_ship(d, source, g).start()

        @pl.when(last)
        def _():
            que_ship(d, source).start()

    def await_ship(d, source, g, last):
        tok_ship(d, source, g).wait_recv()

        @pl.when(last)
        def _():
            que_ship(d, source).wait_recv()

    def project(source, g, last):
        block = (blocks[source, g].astype(f32) * gain).astype(bf16)
        chunk = source * 4 + g
        for d in range(2):
            cols = slice(d * kcols, (d + 1) * kcols)
            parts[d, chunk, :, :kcols] = dot(block, wk[:, cols]).astype(bf16)
            parts[d, chunk, :, kcols:] = dot(block, wv[:, cols]).astype(bf16)

        @pl.when(last)
        def _():
            raw = dot(picks[source], blocks[source].reshape(tokens, width))
            rawrows[source] = raw.astype(bf16)
            taken = (raw * gain).astype(bf16)
            for d in range(2):
                cols = slice(d * qcols, (d + 1) * qcols)
                qparts[d, source] = dot(taken, wq[:, cols]).astype(bf16)

        @pl.when(is_end)
        def _():
            ship(1 - side, source, g, last)

    def combine(d, source, g, last):
        await_ship(d, source, g, last)
        chunk = source * 4 + g
        both = parts[d, chunk].astype(f32) + inbox[d, chunk].astype(f32)
        parts[d, chunk] = both.astype(bf16)

        @pl.when(last)
        def _():
            both = qparts[d, source].astype(f32) + qinbox[d, source].astype(f32)
            qparts[d, source] = both.astype(bf16)

        ship(d, source, g, last)

    chunks = 4 * seq
    order_own = (0, 1, 4, 5, 2, 3, 8, 12, 6, 7, 9, 13, 10, 14, 11, 15)
    order_one = (4, 0, 5, 1, 8, 12, 6, 2, 7, 3, 9, 13, 10, 14, 11, 15)
    order_two = (12, 8, 0, 4, 9, 13, 10, 14, 11, 15, 1, 5, 2, 6, 3, 7)
    order_end = (12, 8, 4, 0, 9, 13, 10, 14, 11, 15, 5, 1, 6, 2, 7, 3)
    lag_one, lag_two = 4, 8

    def step(number, carry):
        @pl.when(number < chunks)
        def _():
            source, g, kind = pick_from(number, order_own)

            @pl.when(jnp.logical_and(kind < 2, source != s))
            def _():
                arrived(source, kind).wait_recv()
                passed(source, kind).start()

            awaits = jnp.logical_not(jnp.logical_and(source == s, home))

            @pl.when(jnp.logical_and(kind >= 2, awaits))
            def _():
                passed(source, kind - 2).wait_recv()

            project(source, g, kind == 3)

        one = number - lag_one

        @pl.when(jnp.logical_and(is_mid, jnp.logical_and(one >= 0, one < chunks)))
        def _():
            source, g, kind = pick_from(one, order_one)
            combine(1 - side, source, g, kind == 3)

        two = number - lag_two

        @pl.when(jnp.logical_and(is_mid, jnp.logical_and(two >= 0, two < chunks)))
        def _():
            source, g, kind = pick_from(two, order_two)
            combine(side, source, g, kind == 3)

        return carry

    lax.fori_loop(0, chunks + lag_two, step, 0)

    def turned(values, cosine, sine):
        return values * cosine + pltpu.roll(values, HEAD_DIM // 2, 1) * sine

    per = seq // 2

    def tell(b, hop):
        peer = {"seq": s + hop * (1 - 2 * side), "tp": t}
        block = att.at[side, b]
        return remote(block, block, asend.at[b, hop], arecv.at[side, b], peer)

    def told_of(source_side, b):
        block = att.at[source_side, b]
        return remote(block, block, asend.at[b, 0], arecv.at[source_side, b], beside)

    def cross(i):
        return remote(away.at[i], arrived_away.at[i], esend.at[i], erecv.at[i], beside)

    length = seq * tokens
    sign = jnp.where(lax.broadcasted_iota(jnp.int32, (1, HEAD_DIM), 1) < HEAD_DIM // 2, -1.0, 1.0)
    kv = kcols // HEAD_DIM
    group = qcols // kcols

    @pl.when(is_end)
    def _():
        def table(b, carry):
            at = pl.ds(pl.multiple_of(b * rows, rows), rows)
            line = lax.broadcasted_iota(jnp.int32, (rows, HEAD_DIM), 0) + b * rows
            angle = line.astype(f32) * freq[...]
            tables[0, at] = jnp.cos(angle)
            tables[1, at] = jnp.sin(angle) * sign
            return carry

        lax.fori_loop(0, length // rows, table, 0)
        angle = rowinfo[0] * freq[...]
        tables[0, length:] = jnp.cos(angle)
        tables[1, length:] = jnp.sin(angle) * sign

        def settle(number, carry):
            source, g, kind = pick_from(number, order_end)
            await_ship(side, source, g, kind == 3)
            chunk = source * 4 + g
            both = parts[side, chunk].astype(f32) + inbox[side, chunk].astype(f32)
            at = pl.ds(pl.multiple_of(chunk * rows, rows), rows)
            cosine, sine = tables[0, at], tables[1, at]
            for j in range(kv):
                key = both[:, j * HEAD_DIM : (j + 1) * HEAD_DIM]
                keys[j, at] = turned(key, cosine, sine).astype(bf16)
                values[j, at] = both[:, kcols + j * HEAD_DIM : kcols + (j + 1) * HEAD_DIM].astype(bf16)

            @pl.when(kind == 3)
            def _():
                both = qparts[side, source].astype(f32) + qinbox[side, source].astype(f32)
                at = pl.ds(pl.multiple_of(source * CAP, CAP), CAP)
                far_at = pl.ds(pl.multiple_of(length + source * CAP, CAP), CAP)
                cosine, sine = tables[0, far_at], tables[1, far_at]
                both = both * rowinfo[3, at][:, 0:1]
                for j in range(kv * group):
                    query = both[:, j * HEAD_DIM : (j + 1) * HEAD_DIM]
                    queries[j, at] = turned(query, cosine, sine).astype(bf16)

            return carry

        lax.fori_loop(0, chunks, settle, 0)
        position = lax.broadcasted_iota(jnp.int32, (1, length), 1).astype(f32)
        scale = scales[0:1, :]
        for which in (other, t):
            at = pl.ds(pl.multiple_of(which * per * CAP, per * CAP), per * CAP)
            row_at, row_start = rowinfo[0, at][:, 0:1], rowinfo[1, at][:, 0:1]
            allowed = jnp.logical_and(position <= row_at, position >= row_start)
            allowed = jnp.logical_and(allowed, row_at - position < float(WINDOW))
            for j in range(kv * group):
                scores = lax.dot_general(
                    queries[j, at], keys[j // group], (((1,), (1,)), ((), ())), preferred_element_type=f32
                )
                scores = jnp.where(allowed, scores * (scale * HEAD_DIM ** (-0.5)), -1e30)
                lifted = jnp.exp(scores - jnp.max(scores, axis=1, keepdims=True))
                lifted = lifted * (1.0 / jnp.sum(lifted, axis=1, keepdims=True))
                result = dot((lifted * scale).astype(bf16), values[j // group]).astype(bf16)
                for b in range(per):
                    cols = slice(j * HEAD_DIM, (j + 1) * HEAD_DIM)
                    att[side, which * per + b, :, cols] = result[b * CAP : (b + 1) * CAP]
            for b in range(per):
                for hop in range(seq - 1, 0, -1):
                    tell(which * per + b, hop).start()

    loads[3].wait()
    late_gain = final_gain[0:1, pl.ds(pl.multiple_of(s * width, width), width)]
    turns = [other * per, other * per + 1, t * per, t * per + 1]
    for k, b in enumerate(turns):
        for source_side in range(2):

            @pl.when(s != (seq - 1) * source_side)
            def _():
                told_of(source_side, b).wait_recv()

        result = dot(att[0, b], wo[:qcols]) + dot(att[1, b], wo[qcols:])
        if k < per:
            away[k] = result.astype(bf16)
            cross(k).start()
        else:
            here[k - per] = result + rawrows[b].astype(f32)

    def along(source, target, i):
        block = fin.at[source, t, i]
        return remote(
            block, block, zsend.at[i, target], zrecv.at[source, i], {"seq": target, "tp": t}
        )

    def across(source, i):
        return remote(
            fin.at[source, t, i], fin.at[source, t, i], bsend.at[source, i], brecv.at[source, i], beside
        )

    fold = []
    for i in range(per):
        cross(i).wait_recv()
        state = here[i] + arrived_away[i].astype(f32)
        fin[s, t, i] = (state * late_gain).astype(bf16)
        across(s, i).start()
        for hop in range(1, seq):
            for d in range(2):
                target = s + hop * (2 * d - 1)

                @pl.when(jnp.logical_and(target >= 0, target < seq))
                def _():
                    along(s, target, i).start()

        total = jnp.zeros((CAP, 128), f32)
        for c in range(width // 128):
            part = state[:, c * 128 : (c + 1) * 128]
            total = total + part * part
        fold.append(total)
    zero = jnp.zeros((CAP, 128), f32)
    lower = t == 0
    fold = [jnp.where(lower, v, zero) for v in fold] + [jnp.where(lower, zero, v) for v in fold]
    total = jnp.concatenate(fold, axis=0)
    squares[...] = jnp.broadcast_to(jnp.sum(total.T, axis=0, keepdims=True), squares.shape)
    sqmessages = tell_all(seq, 2, squares, sqtold, sqsend, sqrecv)
    loads[4].wait()

    def add(source, which, i, fresh):
        at = pl.ds(pl.multiple_of((which * per + i) * CAP, CAP), CAP)
        weight = head[pl.ds(pl.multiple_of(source * width, width), width)]
        value = dot(fin[source, which, i], weight)
        logits[at] = value if fresh else logits[at] + value

    for i in range(per):
        add(s, t, i, True)
    for i in range(per):
        across(s, i).wait_recv()
        add(s, other, i, True)
    for hop in range(1, seq):
        for d in range(2):
            source = s - hop * (2 * d - 1)

            @pl.when(jnp.logical_and(source >= 0, source < seq))
            def _():
                for i in range(per):
                    along(source, s, i).wait_recv()
                    across(source, i).start()
                    add(source, t, i, False)

        for d in range(2):
            source = s - hop * (2 * d - 1)

            @pl.when(jnp.logical_and(source >= 0, source < seq))
            def _():
                for i in range(per):
                    across(source, i).wait_recv()
                    add(source, other, i, False)

    for message in sqmessages:
        message.wait_recv()
    total = jnp.zeros(squares.shape, f32)
    for b in range(seq):
        total = total + sqtold[b, 0] + sqtold[b, 1]
    count = seq * CAP
    mean = jnp.broadcast_to(total[0:1, :], (count, count)).T[:, 0:1] / model
    final = logits[...] * lax.rsqrt(mean + EPS)
    entries = final.shape[1]
    top = jnp.max(final, axis=1, keepdims=True)
    exps = jnp.sum(jnp.exp(final - top), axis=1, keepdims=True)
    label = lax.broadcasted_iota(jnp.int32, (1, entries), 1) + (s * 2 + t) * entries
    found = jnp.sum(
        jnp.where(rowinfo[2][:, 0:1] == label.astype(f32), final, 0.0), axis=1, keepdims=True
    )
    lane = lax.broadcasted_iota(jnp.int32, (count, count), 1)
    packed = jnp.where(lane == 0, top, jnp.where(lane == 1, exps, jnp.where(lane == 2, found, 0.0)))
    stats[...] = packed.T[0:8, :]
    stmessages = tell_all(seq, 2, stats, sttold, stsend, strecv)
    for message in stmessages:
        message.wait_recv()
    everyones = [sttold[b, e] for b in range(seq) for e in range(2)]
    best = everyones[0][0:1, :]
    for value in everyones[1:]:
        best = jnp.maximum(best, value[0:1, :])
    summed = jnp.zeros((1, count), f32)
    hits = jnp.zeros((1, count), f32)
    for value in everyones:
        summed = summed + value[1:2, :] * jnp.exp(value[0:1, :] - best)
        hits = hits + value[2:3, :]
    logp = hits - (best + jnp.log(summed))
    own = picks[s].astype(f32)
    select = jnp.concatenate([jnp.where(s == b, own, 0.0) for b in range(seq)], axis=0)
    column = jnp.broadcast_to(logp, (count, count)).T[:, 0:1]
    out[...] = jnp.sum(select * column, axis=0, keepdims=True)

    for pair in pairs:
        firsts[pair].wait_send()
    for source in range(seq):
        for p in range(2):

            @pl.when(source != s)
            def _():
                arrived(source, p).wait_send()

            @pl.when(jnp.logical_or(source != s, home))
            def _():
                passed(source, p).wait_send()

    for message in messages + sqmessages + stmessages:
        message.wait_send()
    for d in range(2):

        @pl.when(s != (seq - 1) * d)
        def _():
            for source in range(seq):
                for g in range(4):
                    tok_ship(d, source, g).wait_send()
                que_ship(d, source).wait_send()

    @pl.when(is_end)
    def _():
        for b in range(seq):
            for hop in range(1, seq):
                tell(b, hop).wait_send()

    for i in range(per):
        cross(i).wait_send()
        for source in range(seq):
            across(source, i).wait_send()

            @pl.when(source != s)
            def _():
                along(s, source, i).wait_send()


def fused_rows(
    hidden,
    segment_ids,
    targets,
    loss_mask,
    attn_gain,
    final_gain,
    w_query,
    w_key,
    w_value,
    w_out,
    head,
):
    seq = lax.axis_size("seq")
    tokens, features = hidden.shape[1:]
    model = features * 2
    width = w_key.shape[1]
    rows = tokens // 4
    kcols = w_key.shape[2] // 2
    qcols = w_query.shape[2] // 2
    kv = kcols // HEAD_DIM
    entries = head.shape[2]
    count = seq * CAP
    freq = THETA ** (-(np.arange(HEAD_DIM // 2) * 2.0 / HEAD_DIM))
    freq = jnp.asarray(np.concatenate([freq, freq])[None, :].astype(np.float32))
    vmem = pl.BlockSpec(memory_space=pltpu.VMEM)
    hbm = pl.BlockSpec(memory_space=pl.ANY)
    bf16, f32 = jnp.bfloat16, jnp.float32
    dma = pltpu.SemaphoreType.DMA
    return pl.pallas_call(
        functools.partial(fused_kernel, seq),
        out_shape=jax.ShapeDtypeStruct((1, tokens), f32),
        in_specs=[vmem] * 7 + [hbm] * 5,
        out_specs=vmem,
        scratch_shapes=[
            pltpu.VMEM(w_query.shape[1:], bf16),
            pltpu.VMEM(w_key.shape[1:], bf16),
            pltpu.VMEM(w_value.shape[1:], bf16),
            pltpu.VMEM(w_out.shape[1:], bf16),
            pltpu.VMEM(head.shape[1:], bf16),
            pltpu.VMEM((8, tokens), f32),
            pltpu.VMEM((seq, 2, 8, tokens), f32),
            pltpu.VMEM((2, rows, features), bf16),
            pltpu.VMEM((seq, 4, rows, width), bf16),
            pltpu.VMEM((2, 4 * seq, rows, 2 * kcols), bf16),
            pltpu.VMEM((2, 4 * seq, rows, 2 * kcols), bf16),
            pltpu.VMEM((2, seq, CAP, qcols), bf16),
            pltpu.VMEM((2, seq, CAP, qcols), bf16),
            pltpu.VMEM((seq, CAP, tokens), bf16),
            pltpu.VMEM((4, count, 128), f32),
            pltpu.VMEM((8, seq * tokens), f32),
            pltpu.VMEM((2, seq * tokens + count, HEAD_DIM), f32),
            pltpu.VMEM((kv, seq * tokens, HEAD_DIM), bf16),
            pltpu.VMEM((kv, seq * tokens, HEAD_DIM), bf16),
            pltpu.VMEM((qcols // HEAD_DIM, count, HEAD_DIM), bf16),
            pltpu.VMEM((2, seq, CAP, qcols), bf16),
            pltpu.VMEM((seq, CAP, width), bf16),
            pltpu.VMEM((seq // 2, CAP, width), bf16),
            pltpu.VMEM((seq // 2, CAP, width), bf16),
            pltpu.VMEM((seq // 2, CAP, width), f32),
            pltpu.VMEM((seq, 2, seq // 2, CAP, width), bf16),
            pltpu.VMEM((count, entries), f32),
            pltpu.VMEM((8, count), f32),
            pltpu.VMEM((seq, 2, 8, count), f32),
            pltpu.VMEM((8, count), f32),
            pltpu.VMEM((seq, 2, 8, count), f32),
            dma((5,)),
            dma((2, 2)),
            dma((2, 2)),
            dma((seq, 2)),
            dma((seq, 2)),
            dma((seq, 2)),
            dma((seq, 2)),
            dma((2 * seq,)),
            dma((2 * seq,)),
            dma((2, 4 * seq)),
            dma((2, 4 * seq)),
            dma((2, seq)),
            dma((2, seq)),
            dma((seq, seq)),
            dma((2, seq)),
            dma((seq // 2,)),
            dma((seq // 2,)),
            dma((seq // 2, seq)),
            dma((seq, seq // 2)),
            dma((seq, seq // 2)),
            dma((seq, seq // 2)),
            dma((2 * seq,)),
            dma((2 * seq,)),
            dma((2 * seq,)),
            dma((2 * seq,)),
        ],
        compiler_params=pltpu.CompilerParams(collective_id=0, has_side_effects=True),
    )(
        hidden[0],
        segment_ids[None, :],
        loss_mask[None, :],
        targets[None, :],
        freq,
        attn_gain,
        final_gain,
        w_query[0],
        w_key[0],
        w_value[0],
        w_out[0],
        head[0],
    )


def solution(mesh):
    placed = (
        P("ref", ("groups", "seq"), "tp"),
        P(("groups", "seq")),
        P(("groups", "seq")),
        P(("groups", "seq")),
        P("ref", None),
        P("ref", None),
        P("ref", "seq", "tp"),
        P("ref", "seq", "tp"),
        P("ref", "seq", "tp"),
        P("ref", "tp", "seq"),
        P("ref", None, ("seq", "tp")),
    )

    def shards(*args):
        seq, tp = mesh.shape["seq"], mesh.shape["tp"]
        own_heads = args[7].shape[2] // HEAD_DIM
        moves = tp == 2 and seq == 4 and own_heads == seq and args[6].shape[2] == 2 * args[7].shape[2]
        return (fused_rows if moves else gathered_weights)(*args)

    return jax.shard_map(
        shards, mesh=mesh, in_specs=placed, out_specs=P("ref", ("groups", "seq")), check_vma=False
    )
```

time: 165 us -> 111 us (0.67)
  other arithmetic: 17.6 us -> 0 us
  Pallas kernels: 126 us -> 110 us
  matrix products: 10.6 us -> 0 us
  local copies, waits for them, and re-layouts: 6.1 us -> 1.24 us
  waiting for transfers between devices: 4.16 us -> 0 us
    pallas_call x4 -> x1, Pallas kernels: 126 us -> 110 us  [fused_rows(): pl.pallas_call(functools.partial(fused_kernel, seq), out_shape=jax.ShapeD...]
    dot_general x6 -> x0, matrix products: 9.96 us -> none  [the longest x1 3.31 us: moved_rows(): logits = jnp.dot(final, head[0], preferred_element_type=jnp.float32)]
    reduce_sum x10 -> x0, other arithmetic: 6.38 us -> none  [the longest x1 1.88 us: moved_rows(): summed = jnp.sum(parts.astype(jnp.float32), axis=0)]
    another operation x8 -> x0, other arithmetic: 4.73 us -> none
    ppermute x1 -> x0, waiting for transfers between devices: 4.16 us -> none  [moved_rows(): lax.ppermute(away, 'tp', [(0, 1), (1, 0)]).astype(jnp.float32)]
    reshape x4 -> x0, local copies, waits for them, and re-layouts: 2.24 us -> none  [the longest x1 1.24 us: moved_rows(): summed[:, :half, :HEAD_DIM].reshape(length, HEAD_DIM)]
    convert_element_type x7 -> x0, other arithmetic: 1.74 us -> none  [the longest x1 0.76 us: moved_rows(): whole = told[:, 0].astype(jnp.int32)]
  transfers between devices with their start and end apart: 1 -> 0, of which waited for: 1 -> 0; matrix products, arithmetic and copies ran while one was open for 0% -> 0% of each run, Pallas kernels for 0% -> 0%
where the time goes in v1:
time: 111 us
  Pallas kernels  110 us (99%)
  local copies, waits for them, and re-layouts  1.24 us (1%)
    pallas_call x1, Pallas kernels, fused_rows(): pl.pallas_call(functools.partial(fused_kernel, seq), out_shape=jax.ShapeD...  110 us

profile of v1, /device:TPU:0, one launch (start us, length us, event | category | flops | bytes accessed | tf_op | source)
XLA Modules:
  0.0 110.8 jit_solution(1191156454283288553)
XLA Ops:
  0.0 109.5 %shard_map.118 = f32[1,256]{1,0:T(1,128)} custom-call(bf16[256,2048]{1,0:T(8,128)(2,1)} %bitcast.12, s32[1,256]{1,0:T(1,128)} %bitcast.15, s32[1,256]{1,0:T(1,128)} %bitcast.16, s32[1,256]{1,0:T(1,128)} %bitcast.17, f32[1,128]{1,0:T(1,128)} %constant.2.clone.freq, f32[1,4096]{1,0:T(1,128)} %attn_gain.1, f32[1,4096]{1,0:T(1,128)} %final_gain.1, ...), custom_call_target="tpu_custom_call" | custom-call | tf_op jit(solution)/shard_map/pallas_call | solution.py:836
  109.5 1.2 %copy.14 = f32[1,256]{1,0:T(1,128)} copy(f32[1,256]{1,0:T(1,128)} %shard_map.118) | data formatting | bytes 2048

commit v2 on v1

--- a/solution.py
+++ b/solution.py
@@ -260,6 +260,8 @@
     head,
     meta,
     told,
+    sums,
+    sumtold,
     half,
     blocks,
     parts,
@@ -293,6 +295,8 @@
     frecv,
     msend,
     mrecv,
+    usend,
+    urecv,
     csend,
     crecv,
     qsend,
@@ -333,6 +337,11 @@
     for load in loads:
         load.start()
     greet([peer for _, peer in everyone(seq, 2)])
+    meta[0:1, :] = segs[...].astype(f32)
+    meta[1:2, :] = mask[...].astype(f32)
+    meta[2:3, :] = target_ids[...].astype(f32)
+    meta[3:8, :] = jnp.zeros((5, tokens), f32)
+    messages = tell_all(seq, 2, meta, told, msend, mrecv)
 
     def piece(which, p, i):
         at = pl.multiple_of((which * 2 + p) * rows, rows)
@@ -381,13 +390,8 @@
     for c in range(x.shape[1] // 128):
         part = x[:, c * 128 : (c + 1) * 128].astype(f32)
         fold = fold + part * part
-    meta[0:1, :] = segs[...].astype(f32)
-    meta[1:2, :] = mask[...].astype(f32)
-    meta[2:3, :] = target_ids[...].astype(f32)
-    meta[3:4, :] = jnp.sum(fold.T, axis=0, keepdims=True)
-    meta[4:8, :] = jnp.zeros((4, tokens), f32)
-    messages = tell_all(seq, 2, meta, told, msend, mrecv)
-
+    sums[...] = jnp.broadcast_to(jnp.sum(fold.T, axis=0, keepdims=True), sums.shape)
+    summessages = tell_all(seq, 2, sums, sumtold, usend, urecv)
     for p, i in pairs:
         firsts[p, i].wait_recv()
         target = other * 2 + i
@@ -422,14 +426,12 @@
         def column(line):
             return jnp.sum(jnp.where(hit, line, 0.0), axis=1, keepdims=True)
 
-        scale = lax.rsqrt((told[b, 0, 3:4, :] + told[b, 1, 3:4, :]) / model + EPS)
-        scales[0:1, b * tokens : (b + 1) * tokens] = scale
         seg = column(told[b, 0, 0:1, :])
         begin = jnp.zeros((CAP, 1), f32)
         for j in range(SEGMENTS):
             begin = begin + jnp.where(seg == float(j), begins[j], 0.0)
         here_rows = slice(b * CAP, (b + 1) * CAP)
-        info = (column(spot + float(b * tokens)), begin, column(told[b, 0, 2:3, :]), column(scale))
+        info = (column(spot + float(b * tokens)), begin, column(told[b, 0, 2:3, :]))
         for kind, value in enumerate(info):
             rowinfo[kind, here_rows] = jnp.broadcast_to(value, (CAP, 128))
 
@@ -515,11 +517,11 @@
         ship(d, source, g, last)
 
     chunks = 4 * seq
-    order_own = (0, 1, 4, 5, 2, 3, 8, 12, 6, 7, 9, 13, 10, 14, 11, 15)
-    order_one = (4, 0, 5, 1, 8, 12, 6, 2, 7, 3, 9, 13, 10, 14, 11, 15)
-    order_two = (12, 8, 0, 4, 9, 13, 10, 14, 11, 15, 1, 5, 2, 6, 3, 7)
-    order_end = (12, 8, 4, 0, 9, 13, 10, 14, 11, 15, 5, 1, 6, 2, 7, 3)
-    lag_one, lag_two = 4, 8
+    order_own = (0, 12, 1, 2, 4, 13, 3, 5, 14, 8, 6, 15, 9, 7, 10, 11)
+    order_one = (12, 0, 4, 13, 1, 5, 14, 8, 2, 6, 15, 9, 3, 7, 10, 11)
+    order_two = (4, 12, 5, 8, 13, 9, 6, 0, 10, 14, 7, 1, 11, 15, 2, 3)
+    order_end = (0, 12, 1, 8, 13, 9, 2, 4, 10, 14, 3, 5, 11, 15, 6, 7)
+    lag_one, lag_two = 4, 7
 
     def step(number, carry):
         @pl.when(number < chunks)
@@ -557,6 +559,13 @@
 
     lax.fori_loop(0, chunks + lag_two, step, 0)
 
+    for message in summessages:
+        message.wait_recv()
+    for b in range(seq):
+        scale = lax.rsqrt((sumtold[b, 0, 0:1, :] + sumtold[b, 1, 0:1, :]) / model + EPS)
+        scales[0:1, b * tokens : (b + 1) * tokens] = scale
+        value = jnp.sum(picks[b].astype(f32) * scale, axis=1, keepdims=True)
+        rowinfo[3, b * CAP : (b + 1) * CAP] = jnp.broadcast_to(value, (CAP, 128))
     def turned(values, cosine, sine):
         return values * cosine + pltpu.roll(values, HEAD_DIM // 2, 1) * sine
 
@@ -708,25 +717,30 @@
     for i in range(per):
         across(s, i).wait_recv()
         add(s, other, i, True)
-    for hop in range(1, seq):
-        for d in range(2):
-            source = s - hop * (2 * d - 1)
-
-            @pl.when(jnp.logical_and(source >= 0, source < seq))
+    sources = [s - hop * (2 * d - 1) for hop in range(1, seq) for d in range(2)]
+    valid = [jnp.logical_and(source >= 0, source < seq) for source in sources]
+    for i in range(per):
+        for source, good in zip(sources, valid):
+
+            @pl.when(good)
             def _():
-                for i in range(per):
-                    along(source, s, i).wait_recv()
-                    across(source, i).start()
-                    add(source, t, i, False)
-
-        for d in range(2):
-            source = s - hop * (2 * d - 1)
-
-            @pl.when(jnp.logical_and(source >= 0, source < seq))
-            def _():
-                for i in range(per):
-                    across(source, i).wait_recv()
-                    add(source, other, i, False)
+                along(source, s, i).wait_recv()
+                across(source, i).start()
+
+    for source, good in zip(sources, valid):
+
+        @pl.when(good)
+        def _():
+            for i in range(per):
+                add(source, t, i, False)
+
+    for source, good in zip(sources, valid):
+
+        @pl.when(good)
+        def _():
+            for i in range(per):
+                across(source, i).wait_recv()
+                add(source, other, i, False)
 
     for message in sqmessages:
         message.wait_recv()
@@ -777,7 +791,7 @@
             def _():
                 passed(source, p).wait_send()
 
-    for message in messages + sqmessages + stmessages:
+    for message in messages + summessages + sqmessages + stmessages:
         message.wait_send()
     for d in range(2):
 
@@ -846,6 +860,8 @@
             pltpu.VMEM(head.shape[1:], bf16),
             pltpu.VMEM((8, tokens), f32),
             pltpu.VMEM((seq, 2, 8, tokens), f32),
+            pltpu.VMEM((8, tokens), f32),
+            pltpu.VMEM((seq, 2, 8, tokens), f32),
             pltpu.VMEM((2, rows, features), bf16),
             pltpu.VMEM((seq, 4, rows, width), bf16),
             pltpu.VMEM((2, 4 * seq, rows, 2 * kcols), bf16),
@@ -879,6 +895,8 @@
             dma((seq, 2)),
             dma((2 * seq,)),
             dma((2 * seq,)),
+            dma((2 * seq,)),
+            dma((2 * seq,)),
             dma((2, 4 * seq)),
             dma((2, 4 * seq)),
             dma((2, seq)),

time: 111 us -> 104 us (0.937)
  Pallas kernels: 110 us -> 103 us
    pallas_call x1, Pallas kernels: 110 us -> 103 us  [fused_rows(): pl.pallas_call(functools.partial(fused_kernel, seq), out_shape=jax.ShapeD...]
where the time goes in v2:
time: 104 us
  Pallas kernels  103 us (99%)
  local copies, waits for them, and re-layouts  1.24 us (1%)
    pallas_call x1, Pallas kernels, fused_rows(): pl.pallas_call(functools.partial(fused_kernel, seq), out_shape=jax.ShapeD...  103 us

profile of v2, /device:TPU:0, one launch (start us, length us, event | category | flops | bytes accessed | tf_op | source)
XLA Modules:
  0.0 104.1 jit_solution(6454696926642494557)
XLA Ops:
  0.0 102.9 %shard_map.118 = f32[1,256]{1,0:T(1,128)} custom-call(bf16[256,2048]{1,0:T(8,128)(2,1)} %bitcast.12, s32[1,256]{1,0:T(1,128)} %bitcast.15, s32[1,256]{1,0:T(1,128)} %bitcast.16, s32[1,256]{1,0:T(1,128)} %bitcast.17, f32[1,128]{1,0:T(1,128)} %constant.2.clone.freq, f32[1,4096]{1,0:T(1,128)} %attn_gain.1, f32[1,4096]{1,0:T(1,128)} %final_gain.1, ...), custom_call_target="tpu_custom_call" | custom-call | tf_op jit(solution)/shard_map/pallas_call | solution.py:850
  102.9 1.2 %copy.14 = f32[1,256]{1,0:T(1,128)} copy(f32[1,256]{1,0:T(1,128)} %shard_map.118) | data formatting | bytes 2048

commit v3 on v2

--- a/solution.py
+++ b/solution.py
@@ -674,6 +674,12 @@
             block, block, zsend.at[i, target], zrecv.at[source, i], {"seq": target, "tp": t}
         )
 
+    def onward(i):
+        block = fin.at[far, t, i]
+        return remote(
+            block, block, zsend.at[i, seq], zrecv.at[far, i], {"seq": partner, "tp": t}
+        )
+
     def across(source, i):
         return remote(
             fin.at[source, t, i], fin.at[source, t, i], bsend.at[source, i], brecv.at[source, i], beside
@@ -685,7 +691,7 @@
         state = here[i] + arrived_away[i].astype(f32)
         fin[s, t, i] = (state * late_gain).astype(bf16)
         across(s, i).start()
-        for hop in range(1, seq):
+        for hop in range(1, seq - 1):
             for d in range(2):
                 target = s + hop * (2 * d - 1)
 
@@ -706,41 +712,44 @@
     sqmessages = tell_all(seq, 2, squares, sqtold, sqsend, sqrecv)
     loads[4].wait()
 
-    def add(source, which, i, fresh):
-        at = pl.ds(pl.multiple_of((which * per + i) * CAP, CAP), CAP)
+    def add(source, which, fresh):
+        at = pl.ds(pl.multiple_of(which * per * CAP, per * CAP), per * CAP)
         weight = head[pl.ds(pl.multiple_of(source * width, width), width)]
-        value = dot(fin[source, which, i], weight)
+        value = dot(fin[source, which].reshape(per * CAP, width), weight)
         logits[at] = value if fresh else logits[at] + value
 
-    for i in range(per):
-        add(s, t, i, True)
-    for i in range(per):
-        across(s, i).wait_recv()
-        add(s, other, i, True)
     sources = [s - hop * (2 * d - 1) for hop in range(1, seq) for d in range(2)]
     valid = [jnp.logical_and(source >= 0, source < seq) for source in sources]
+    add(s, t, True)
     for i in range(per):
         for source, good in zip(sources, valid):
 
             @pl.when(good)
             def _():
                 along(source, s, i).wait_recv()
+
+                @pl.when(jnp.logical_and(is_mid, source == far))
+                def _():
+                    onward(i).start()
+
                 across(source, i).start()
 
     for source, good in zip(sources, valid):
 
         @pl.when(good)
         def _():
-            for i in range(per):
-                add(source, t, i, False)
-
+            add(source, t, False)
+
+    for i in range(per):
+        across(s, i).wait_recv()
+    add(s, other, True)
     for source, good in zip(sources, valid):
 
         @pl.when(good)
         def _():
             for i in range(per):
                 across(source, i).wait_recv()
-                add(source, other, i, False)
+            add(source, other, False)
 
     for message in sqmessages:
         message.wait_recv()
@@ -813,9 +822,13 @@
         for source in range(seq):
             across(source, i).wait_send()
 
-            @pl.when(source != s)
+            @pl.when(jnp.logical_and(source != s, jnp.abs(source - s) < seq - 1))
             def _():
                 along(s, source, i).wait_send()
+
+        @pl.when(is_mid)
+        def _():
+            onward(i).wait_send()
 
 
 def fused_rows(
@@ -905,7 +918,7 @@
             dma((2, seq)),
             dma((seq // 2,)),
             dma((seq // 2,)),
-            dma((seq // 2, seq)),
+            dma((seq // 2, seq + 1)),
             dma((seq, seq // 2)),
             dma((seq, seq // 2)),
             dma((seq, seq // 2)),

time: 104 us -> 103 us (level)
    pallas_call x1, Pallas kernels: 103 us -> 102 us  [fused_rows(): pl.pallas_call(functools.partial(fused_kernel, seq), out_shape=jax.ShapeD...]
where the time goes in v3:
time: 103 us
  Pallas kernels  102 us (99%)
  local copies, waits for them, and re-layouts  1.24 us (1%)
    pallas_call x1, Pallas kernels, fused_rows(): pl.pallas_call(functools.partial(fused_kernel, seq), out_shape=jax.ShapeD...  102 us

profile of v3, /device:TPU:0, one launch (start us, length us, event | category | flops | bytes accessed | tf_op | source)
XLA Modules:
  0.0 102.8 jit_solution(11360249064612795315)
XLA Ops:
  0.0 101.6 %shard_map.118 = f32[1,256]{1,0:T(1,128)} custom-call(bf16[256,2048]{1,0:T(8,128)(2,1)} %bitcast.12, s32[1,256]{1,0:T(1,128)} %bitcast.15, s32[1,256]{1,0:T(1,128)} %bitcast.16, s32[1,256]{1,0:T(1,128)} %bitcast.17, f32[1,128]{1,0:T(1,128)} %constant.2.clone.freq, f32[1,4096]{1,0:T(1,128)} %attn_gain.1, f32[1,4096]{1,0:T(1,128)} %final_gain.1, ...), custom_call_target="tpu_custom_call" | custom-call | tf_op jit(solution)/shard_map/pallas_call | solution.py:863
  101.6 1.2 %copy.14 = f32[1,256]{1,0:T(1,128)} copy(f32[1,256]{1,0:T(1,128)} %shard_map.118) | data formatting | bytes 2048
